TPU v7x, 16 devices: a whole 2x2x2 slice. The times are simulated.
16 devices in a mesh: dp: 2 (over z), tp: 8 (over y, x, core).
Axes of the slice: x: 2, y: 2, z: 2, core: 2. Of those that a mesh axis runs over, the one named last changes fastest.
Arguments:
- x: bfloat16 [512, 2048], P('dp'), parts along dimension 0
- ln_attn_gamma: float32 [2048], replicated
- ln_attn_beta: float32 [2048], replicated
- ln_mlp_gamma: float32 [2048], replicated
- ln_mlp_beta: float32 [2048], replicated
- w_qkv: bfloat16 [2048, 16, 3, 128], P(None, 'tp')
- w_out: bfloat16 [16, 1, 128, 2048], P('tp')
- w_up: bfloat16 [2048, 8192], P(None, 'tp')
- w_down: bfloat16 [8192, 2048], P('tp')
- k_cache: bfloat16 [512, 16, 128, 128], P('dp', 'tp'), parts along dimension 0
- v_cache: bfloat16 [512, 16, 128, 128], P('dp', 'tp'), parts along dimension 0
- positions: int32 [512], P('dp'), parts along dimension 0
Outputs:
- output 1: bfloat16 [512, 2048], P('dp'), parts along dimension 0
- output 2: bfloat16 [512, 16, 128, 128], P('dp', 'tp'), parts along dimension 0
- output 3: bfloat16 [512, 16, 128, 128], P('dp', 'tp'), parts along dimension 0
There are 2 independent parts. A program takes and returns all parts, laid end to end along the dimension named above; an argument that names none is the same for every part.
All inputs are finite; a program needn't handle non-finite values.
Results may differ from a plain program's by a relative error of at most 0.0110548.
Values are sent between devices in bfloat16 or wider.
A program may use at most 1 GiB of HBM per device.

v0:
```python
import jax
import jax.numpy as jnp
from jax import lax
from jax.sharding import PartitionSpec as P

LN_EPS = 1e-5
ROPE_BASE = 10000.0
NEG_BIG = -1e30


def layer_norm(act_rows, ln_gamma, ln_beta):
    rows_f32 = act_rows.astype(jnp.float32)
    row_mean = jnp.mean(rows_f32, axis=-1, keepdims=True)
    centred = rows_f32 - row_mean
    row_var = jnp.mean(centred * centred, axis=-1, keepdims=True)
    return (centred * lax.rsqrt(row_var + LN_EPS) * ln_gamma + ln_beta).astype(jnp.bfloat16)


def apply_rotary(vectors, cos_t, sin_t):
    half_width = vectors.shape[-1] // 2
    as_f32 = vectors.astype(jnp.float32)
    lower_half = as_f32[..., :half_width]
    upper_half = as_f32[..., half_width:]
    return jnp.concatenate([lower_half * cos_t - upper_half * sin_t, upper_half * cos_t + lower_half * sin_t], axis=-1).astype(jnp.bfloat16)


def attend_local(attn_in, w_qkv, k_cache, v_cache, positions):
    n_query = w_qkv.shape[2] - 2
    head_dim = w_qkv.shape[3]
    qkv_rows = jnp.einsum('bd,dgjh->bgjh', attn_in, w_qkv, preferred_element_type=jnp.float32).astype(jnp.bfloat16)
    inv_freq = ROPE_BASE ** (-2.0 * jnp.arange(head_dim // 2, dtype=jnp.float32) / head_dim)
    angles = positions.astype(jnp.float32)[:, None] * inv_freq[None, :]
    cos_t = jnp.cos(angles)
    sin_t = jnp.sin(angles)
    queries = apply_rotary(qkv_rows[:, :, :n_query], cos_t[:, None, None, :], sin_t[:, None, None, :])
    new_key = apply_rotary(qkv_rows[:, :, n_query], cos_t[:, None, :], sin_t[:, None, :])
    new_value = qkv_rows[:, :, n_query + 1]
    slot_ids = jnp.arange(k_cache.shape[2])
    write_mask = (slot_ids[None, :] == positions[:, None])[:, None, :, None]
    keys_all = jnp.where(write_mask, new_key[:, :, None, :], k_cache)
    values_all = jnp.where(write_mask, new_value[:, :, None, :], v_cache)
    valid_mask = (slot_ids[None, :] <= positions[:, None])[:, None, None, :]
    scores = jnp.einsum('bgqh,bgsh->bgqs', queries, keys_all, preferred_element_type=jnp.float32) * (head_dim ** -0.5)
    scores = jnp.where(valid_mask, scores, NEG_BIG)
    attn_probs = jax.nn.softmax(scores, axis=-1).astype(jnp.bfloat16)
    context = jnp.einsum('bgqs,bgsh->bgqh', attn_probs, values_all, preferred_element_type=jnp.float32).astype(jnp.bfloat16)
    return context, keys_all, values_all


def solution(mesh):
    row_spec = P('dp', None)
    vec_spec = P(None)
    cache_spec = P('dp', 'tp', None, None)

    def device_step(x, ln_attn_gamma, ln_attn_beta, ln_mlp_gamma, ln_mlp_beta, w_qkv, w_out, w_up, w_down, k_cache, v_cache, positions):
        attn_in = layer_norm(x, ln_attn_gamma, ln_attn_beta)
        mlp_in = layer_norm(x, ln_mlp_gamma, ln_mlp_beta)
        context, keys_all, values_all = attend_local(attn_in, w_qkv, k_cache, v_cache, positions)
        attn_part = jnp.einsum('bgqh,gqhd->bd', context, w_out, preferred_element_type=jnp.float32).astype(jnp.bfloat16)
        attn_total = lax.psum(attn_part, 'tp')
        hidden = jax.nn.gelu(jnp.dot(mlp_in, w_up, preferred_element_type=jnp.float32), approximate=False).astype(jnp.bfloat16)
        mlp_part = jnp.dot(hidden, w_down, preferred_element_type=jnp.float32).astype(jnp.bfloat16)
        mlp_total = lax.psum(mlp_part, 'tp')
        layer_out = (x.astype(jnp.float32) + attn_total.astype(jnp.float32) + mlp_total.astype(jnp.float32)).astype(jnp.bfloat16)
        return layer_out, keys_all, values_all

    return jax.shard_map(device_step, mesh=mesh, in_specs=(row_spec, vec_spec, vec_spec, vec_spec, vec_spec, P(None, 'tp', None, None), P('tp', None, None, None), P(None, 'tp'), P('tp', None), cache_spec, cache_spec, P('dp')), out_specs=(row_spec, cache_spec, cache_spec), check_vma=False)
```

profile of v0, /device:TPU:0, one launch (start us, length us, event | category | flops | bytes accessed | tf_op | source)
XLA Modules:
  0.0 145.5 jit_solution(14818348021589417878)
XLA Ops:
  7.2 0.0 copy-start
  7.2 0.0 all-reduce.3.cloned.1.call-start
  7.2 0.8 convert_element_type.65
  8.0 0.8 iota_compare_fusion.1
  8.8 1.4 convert_reduce_fusion
  10.2 1.6 %fusion.11 = f32[256]{0:T(256)S(1)} fusion(bf16[256,2048]{1,0:T(8,128)(2,1)} %param.12, f32[256]{0:T(256)S(1)} %broadcast_multiply_fusion), kind=kLoop, calls=%fused_computation.18 | loop fusion | flops 2096896 | bytes 1050624 | tf_op jit(solution)/shard_map/reduce_sum | solution.py:15
  11.9 0.0 copy-start.1
  11.9 8.7 %copy.22 = bf16[2048,2,3,128]{0,3,2,1:T(8,128)(2,1)} copy(bf16[2048,2,3,128]{3,1,2,0:T(2,128)(2,1)} %param.17) | data formatting | bytes 6291456 | tf_op args[5]
  20.7 3.0 %fusion.24 = f32[256,768]{0,1:S(1)} fusion(bf16[2048,768]{0,1:T(8,128)(2,1)} %bitcast.64, bf16[256,2048]{1,0:T(8,128)(2,1)S(1)} %copy-done.1, f32[2048]{0:T(1024)S(1)} %copy-done.2, f32[2048]{0:T(1024)S(1)} %copy-done.3, f32[256]{0:T(256)S(1)} %add_rsqrt_fusion, f32[256]{0:T(256)S(1)} %broadcast_multiply_fusion), kind=kOutput, calls=%fused_computation.31 | convolution fusion | flops 808452096 | bytes 4999168
  23.8 0.1 fusion.81
  23.8 0.3 multiply_cosine_fusion
  24.3 0.1 copy.27
  24.4 0.2 copy.29
  24.6 0.1 copy.28
  24.7 23.0 %broadcast_select_fusion.1 = (bf16[256,2,128,128]{3,2,1,0:T(8,128)(2,1)}, bf16[256,2,128,128]{3,2,1,0:T(8,128)(2,1)}) fusion(bf16[256,2,128,128]{3,2,1,0:T(8,128)(2,1)} %param.21, pred[256,128]{1,0:T(8,128)(4,1)S(1)} %get-tuple-element.16, bf16[256,2,128]{2,1,0:T(2,128)(2,1)S(1)} %copy.27, bf16[256,2,128,128]{3,2,1,0:T(8,128)(2,1)} %param.22, ...), kind=kLoop, calls=%fused_computation.3 | loop fusion | flops 16777216 | bytes 67403776 | tf_op jit(solution)/shard_map/jit(_where)/select_n | solution.py:40
  47.8 12.2 %fusion.130 = f32[256,2,1,128]{3,2,1,0:T(1,128)S(1)} fusion(bf16[256,2,128,1]{2,3,1,0:T(2,128)(2,1)S(1)} %copy.29, bf16[256,2,128,128]{3,2,1,0:T(8,128)(2,1)} %get-tuple-element.11), kind=kOutput, calls=%fused_computation.154 | convolution fusion | flops 16777216 | bytes 17170432 | tf_op jit(solution)/shard_map/bgqh,bgsh->bgqs/dot_general | solution.py:43
  60.0 0.3 fusion.18
  60.3 0.0 copy-start.5
  60.3 8.1 %fusion.77 = bf16[256,2,1,128]{3,2,1,0:T(2,128)(2,1)S(1)} fusion(bf16[256,2,128,128]{3,2,1,0:T(8,128)(2,1)} %get-tuple-element.12, bf16[256,2,128,1]{2,0,1,3:T(8,128)(2,1)S(1)} %fusion.18), kind=kOutput, calls=%fused_computation.89 | convolution fusion | flops 16777216 | bytes 17039360 | tf_op jit(solution)/shard_map/bgqs,bgsh->bgqh/dot_general | solution.py:46
  68.3 1.4 fusion.2
  69.8 9.0 %convolution_convert_fusion = bf16[256,2048]{1,0:T(8,128)(2,1)} fusion(bf16[1024,2048]{1,0:T(8,128)(2,1)} %param.20, bf16[2048,1024]{1,0:T(8,128)(2,1)} %param.19, bf16[256,2048]{1,0:T(8,128)(2,1)S(1)} %copy-done.1, f32[2048]{0:T(1024)S(1)} %copy-done.4, f32[2048]{0:T(1024)S(1)} %copy-done.5, f32[256]{0:T(256)S(1)} %add_rsqrt_fusion, ...), kind=kOutput, calls=%fused_computation.9 | convolution fusion | flops 2168193024 | bytes 10504192 | tf_op jit(solution)/shard_map/dot_general | solution.py:62
  78.8 0.0 all-reduce.3.cloned.1.call-update
  78.8 56.7 %all-reduce.3.cloned.1.call-done = (bf16[256,2048]{1,0:T(8,128)(2,1)}, bf16[256,2048]{1,0:T(8,128)(2,1)}) async-done(((bf16[256,2048]{1,0:T(8,128)(2,1)}, bf16[256,2048]{1,0:T(8,128)(2,1)}), (bf16[256,2048]{1,0:T(8,128)(2,1)}, bf16[256,2048]{1,0:T(8,128)(2,1)})) %all-reduce.3.cloned.1.call-update) | async-done | bytes 2097168 | tf_op jit(solution)/shard_map/psum | solution.py:63
  135.6 3.1 %fusion.13 = bf16[256,2048]{1,0:T(8,128)(2,1)} fusion(bf16[256,2048]{1,0:T(8,128)(2,1)S(1)} %copy-done.1, bf16[256,2048]{1,0:T(8,128)(2,1)} %get-tuple-element.3, bf16[256,2048]{1,0:T(8,128)(2,1)} %get-tuple-element.4), kind=kLoop, calls=%fused_computation.20 | loop fusion | flops 3145728 | bytes 4194304 | tf_op jit(solution)/shard_map/convert_element_type | solution.py:64
  (18 shorter events, 0.2 us)
Async XLA Ops:
  7.2 61.2 %copy-start = (bf16[2,1,128,2048]{3,2,1,0:T(8,128)(2,1)S(1)}, bf16[2,1,128,2048]{3,2,1,0:T(8,128)(2,1)}, u32[]{:S(2)}) copy-start(bf16[2,1,128,2048]{3,2,1,0:T(8,128)(2,1)} %param.18) | copy-start | bytes 3145732
  7.2 128.4 %all-reduce.3.cloned.1.call-start = ((), (), s32[]{:S(2)}) async-start(), calls=%async_computation | async-start | bytes 4194304 | tf_op jit(solution)/shard_map/psum | solution.py:63
  11.9 8.8 %copy-start.1 = (bf16[256,2048]{1,0:T(8,128)(2,1)S(1)}, bf16[256,2048]{1,0:T(8,128)(2,1)}, u32[]{:S(2)}) copy-start(bf16[256,2048]{1,0:T(8,128)(2,1)} %param.12) | copy-start | bytes 3145732
  11.9 8.7 %copy-start.2 = (f32[2048]{0:T(1024)S(1)}, f32[2048]{0:T(1024)}, u32[]{:S(2)}) copy-start(f32[2048]{0:T(1024)} %param.14) | copy-start | bytes 24580
  11.9 8.7 %copy-start.3 = (f32[2048]{0:T(1024)S(1)}, f32[2048]{0:T(1024)}, u32[]{:S(2)}) copy-start(f32[2048]{0:T(1024)} %param.13) | copy-start | bytes 24580
  60.2 9.5 %copy-start.4 = (f32[2048]{0:T(1024)S(1)}, f32[2048]{0:T(1024)}, u32[]{:S(2)}) copy-start(f32[2048]{0:T(1024)} %param.16) | copy-start | bytes 24580
  60.3 9.5 %copy-start.5 = (f32[2048]{0:T(1024)S(1)}, f32[2048]{0:T(1024)}, u32[]{:S(2)}) copy-start(f32[2048]{0:T(1024)} %param.15) | copy-start | bytes 24580
Sparse Core Ops, SparseCore 0:
  79.0 56.5 all-reduce.2
where the time goes:
time: 146 us; the launch traced here: 145 us
  waiting for transfers between devices  56.8 us (39%)
  matrix products  33.8 us (23%)
  other arithmetic  31.5 us (22%)
  between operations  14.2 us (10%)
  local copies, waits for them, and re-layouts  9.15 us (6%)
    psum x1, waiting for transfers between devices, device_step(): mlp_total = lax.psum(mlp_part, 'tp')  56.7 us
    select_n x1, other arithmetic, attend_local(): keys_all = jnp.where(write_mask, new_key[:, :, None, :], k_cache)  23 us
    dot_general x1, matrix products, attend_local(): jnp.einsum('bgqh,bgsh->bgqs', queries, keys_all, preferred_element_type=j...  12.2 us
    dot_general x1, matrix products, device_step(): jnp.dot(hidden, w_down, preferred_element_type=jnp.float32)  9.04 us
    unnamed x13, local copies, waits for them, and re-layouts  8.76 us
    dot_general x1, matrix products, attend_local(): jnp.einsum('bgqs,bgsh->bgqh', attn_probs, values_all, preferred_element_t...  8.06 us
    convert_element_type x1, other arithmetic, device_step(): (x.astype(jnp.float32) + attn_total.astype(jnp.float32) + mlp_total.astyp...  3.05 us
    unnamed x1, matrix products  3.04 us
  transfers between devices with their start and end apart: 1, of which 1 were waited for; matrix products, arithmetic and copies ran while one was open for 0% of the time, Pallas kernels for 0%

commit v1 on v0

v1 whole, which is shorter than its diff:
```python
import functools
import math

import jax
import jax.numpy as jnp
import numpy as np
from jax import lax
from jax.experimental import pallas as pl
from jax.experimental.pallas import tpu as pltpu
from jax.sharding import PartitionSpec as P

LN_EPS = 1e-5
ROPE_BASE = 10000.0
NEG_BIG = -1e30
MESH = pl.DeviceIdType.MESH
F32 = jnp.float32
BF16 = jnp.bfloat16
ROWS = 16
CONTRACT_LAST = (((1,), (1,)), ((), ()))


def quad_lhs(block, tile):
    row = lax.broadcasted_iota(jnp.int32, block.shape, 0)
    zero = jnp.zeros_like(block)
    left = jnp.where((row == 4 * tile) | (row == 4 * tile + 2), block, zero)
    right = jnp.where((row == 4 * tile + 1) | (row == 4 * tile + 3), block, zero)
    return jnp.concatenate([left, right], axis=1).astype(BF16)


def pick_half(acc):
    row = lax.broadcasted_iota(jnp.int32, (acc.shape[0], 128), 0)
    return jnp.where((row & 3) < 2, acc[:, :128], acc[:, 128:])


def layer_kernel(x_hbm, g1_hbm, b1_hbm, g2_hbm, b2_hbm, freq_hbm, wqkv_hbm, wout_hbm, wup_hbm, wdown_hbm, k_hbm, v_hbm, pos_hbm,
                 part_ref, ko_hbm, vo_hbm,
                 x_ref, ln_ref, freq_ref, wraw_ref, wcat_ref, wout_ref, wup_ref, wdown_ref, kbuf, vbuf, pos_ref,
                 ain_ref, min_ref, y_ref, t_ref, q_ref, nk_ref, nv_ref, s_ref, ctx_ref, hid_ref, stage_ref,
                 sem_in, sem_w, sem_k, sem_v, sem_ko, sem_vo):
    n_rows, d_model = x_ref.shape
    n_groups = kbuf.shape[1]
    n_chunks = n_rows // ROWS
    n_wparts = 4
    wrows = wraw_ref.shape[0] // n_wparts

    def copy_small(i, src, dst):
        return pltpu.make_async_copy(src, dst, sem_in.at[i])

    smalls = [copy_small(0, pos_hbm, pos_ref), copy_small(1, x_hbm, x_ref), copy_small(2, freq_hbm, freq_ref)]
    for i, src in enumerate((g1_hbm, b1_hbm, g2_hbm, b2_hbm)):
        smalls.append(copy_small(3 + i, src, ln_ref.at[i]))
    for c in smalls:
        c.start()
    wparts = [pltpu.make_async_copy(wqkv_hbm.at[pl.ds(i * wrows, wrows)], wraw_ref.at[pl.ds(i * wrows, wrows)], sem_w.at[i])
              for i in range(n_wparts)]
    for c in wparts:
        c.start()

    def chunk_ds(i):
        return pl.ds(pl.multiple_of(i * ROWS, ROWS), ROWS)

    def k_in(i):
        return pltpu.make_async_copy(k_hbm.at[chunk_ds(i)], kbuf.at[chunk_ds(i)], sem_k.at[i])

    def v_in(i):
        return pltpu.make_async_copy(v_hbm.at[chunk_ds(i)], vbuf.at[chunk_ds(i)], sem_v.at[i])

    def k_out(i):
        return pltpu.make_async_copy(kbuf.at[chunk_ds(i)], ko_hbm.at[chunk_ds(i)], sem_ko.at[i])

    def v_out(i):
        return pltpu.make_async_copy(vbuf.at[chunk_ds(i)], vo_hbm.at[chunk_ds(i)], sem_vo.at[i])

    for i in range(n_chunks):
        k_in(i).start()
        v_in(i).start()
    wbig = [pltpu.make_async_copy(wup_hbm, wup_ref, sem_w.at[n_wparts]),
            pltpu.make_async_copy(wdown_hbm, wdown_ref, sem_w.at[n_wparts + 1]),
            pltpu.make_async_copy(wout_hbm, wout_ref, sem_w.at[n_wparts + 2])]
    for c in wbig:
        c.start()

    smalls[0].wait()
    row8 = lax.broadcasted_iota(jnp.int32, (8, 128), 0)

    @pl.loop(0, n_rows // 8)
    def _(r):
        tile = jnp.zeros((8, 128), jnp.int32)
        for j in range(8):
            tile = jnp.where(row8 == j, pos_ref[r * 8 + j], tile)
        t_ref[pl.ds(pl.multiple_of(r * 8, 8), 8), :] = tile

    for c in smalls[1:]:
        c.wait()

    gains = [ln_ref[i] for i in range(4)]

    @pl.loop(0, n_rows // 16)
    def _(r):
        rows = pl.ds(pl.multiple_of(r * 16, 16), 16)
        act = x_ref[rows, :].astype(F32)
        mean = jnp.mean(act, axis=-1, keepdims=True)
        centred = act - mean
        var = jnp.mean(centred * centred, axis=-1, keepdims=True)
        normed = centred * lax.rsqrt(var + LN_EPS)
        ain_ref[rows, :] = (normed * gains[0] + gains[1]).astype(BF16)
        min_ref[rows, :] = (normed * gains[2] + gains[3]).astype(BF16)

    depth = 64
    n_split = 3 * n_groups
    for p in range(n_wparts):
        wparts[p].wait()

        @pl.loop(0, wrows // (depth * n_split))
        def _(r):
            first = p * wrows + r * (depth * n_split)
            stage_ref[...] = wraw_ref[pl.ds(pl.multiple_of(first, depth * n_split), depth * n_split), :].astype(F32)
            feat = pl.ds(pl.multiple_of(p * (wrows // n_split) + r * depth, depth), depth)
            for slot in range(3):
                for g in range(n_groups):
                    col = (g * 3 + slot) * 128
                    wcat_ref[feat, col:col + 128] = stage_ref[pl.ds(slot * n_groups + g, depth, stride=n_split), :].astype(BF16)

    for c0 in range(0, 3 * n_groups * 128, 256):
        y_ref[:, c0:c0 + 256] = jnp.dot(ain_ref[...], wcat_ref[:, c0:c0 + 256], preferred_element_type=F32).astype(BF16).astype(F32)

    angles = t_ref[...].astype(F32) * freq_ref[...]
    cos_t = jnp.cos(angles)
    lane = lax.broadcasted_iota(jnp.int32, angles.shape, 1)
    sin_t = jnp.sin(angles)
    sin_t = jnp.where(lane < 64, -sin_t, sin_t)
    for g in range(n_groups):
        for slot, dst in ((0, q_ref), (1, nk_ref)):
            vec = y_ref[:, (g * 3 + slot) * 128:(g * 3 + slot + 1) * 128]
            turned = vec * cos_t + pltpu.roll(vec, 64, 1) * sin_t
            dst[g] = turned.astype(BF16).astype(F32)
        nv_ref[g] = y_ref[:, (g * 3 + 2) * 128:(g * 3 + 3) * 128]

    slot16 = lax.broadcasted_iota(jnp.int32, (128, 128), 0).astype(F32).astype(BF16).reshape(8, 16, 128)
    scale = 128 ** -0.5

    def put_new(buf, i, b, g, new16, pos16):
        old = buf[i * ROWS + b, g].reshape(8, 16, 128)
        new = jnp.broadcast_to(new16[b:b + 1, :], (16, 128)).astype(BF16)[None]
        at = jnp.broadcast_to(pos16[b:b + 1, :], (16, 128)).astype(BF16)[None]
        block = jnp.where(slot16 == at, new, old).reshape(128, 128)
        buf[i * ROWS + b, g] = block
        return block

    def score_chunk(i):
        k_in(i).wait()
        rows = chunk_ds(i)
        pos16 = t_ref[rows, :].astype(F32)
        for g in range(n_groups):
            new16 = nk_ref[g, rows, :]
            q16 = q_ref[g, rows, :]
            acc = None
            for tile in range(4):
                blk = [put_new(kbuf, i, 4 * tile + j, g, new16, pos16) for j in range(4)]
                rhs = jnp.concatenate([jnp.concatenate(blk[:2], axis=1), jnp.concatenate(blk[2:], axis=1)], axis=0)
                part = lax.dot_general(quad_lhs(q16, tile), rhs, CONTRACT_LAST, preferred_element_type=F32)
                acc = part if acc is None else acc + part
            s_ref[i % 2, g] = pick_half(acc) * scale
        k_out(i).start()

    def context_chunk(i):
        v_in(i).wait()
        rows = chunk_ds(i)
        pos16 = t_ref[rows, :]
        lane16 = lax.broadcasted_iota(jnp.int32, (ROWS, 128), 1)
        pos16f = pos16.astype(F32)
        for g in range(n_groups):
            sc = jnp.where(lane16 <= pos16, s_ref[i % 2, g], NEG_BIG)
            ex = jnp.exp(sc - jnp.max(sc, axis=-1, keepdims=True))
            prob = (ex / jnp.sum(ex, axis=-1, keepdims=True)).astype(BF16).astype(F32)
            new16 = nv_ref[g, rows, :]
            acc = None
            for tile in range(4):
                blk = [put_new(vbuf, i, 4 * tile + j, g, new16, pos16f) for j in range(4)]
                rhs = jnp.concatenate([jnp.concatenate(blk[0::2], axis=1), jnp.concatenate(blk[1::2], axis=1)], axis=0)
                part = jnp.dot(quad_lhs(prob, tile), rhs, preferred_element_type=F32)
                acc = part if acc is None else acc + part
            ctx_ref[rows, g * 128:(g + 1) * 128] = pick_half(acc).astype(BF16)
        v_out(i).start()

    score_chunk(0)

    @pl.loop(1, n_chunks)
    def _(i):
        score_chunk(i)
        context_chunk(i - 1)

    context_chunk(n_chunks - 1)

    wbig[0].wait()

    @pl.loop(0, wup_ref.shape[1] // 256)
    def _(c):
        cols = pl.ds(pl.multiple_of(c * 256, 256), 256)
        up = jnp.dot(min_ref[...], wup_ref[:, cols], preferred_element_type=F32)
        hid_ref[:, cols] = (0.5 * up * (1.0 + lax.erf(up * math.sqrt(0.5)))).astype(BF16)

    wbig[1].wait()
    wbig[2].wait()

    @pl.loop(0, d_model // 256)
    def _(c):
        cols = pl.ds(pl.multiple_of(c * 256, 256), 256)
        total = jnp.dot(hid_ref[...], wdown_ref[:, cols], preferred_element_type=F32)
        total = total + jnp.dot(ctx_ref[...], wout_ref[:, cols], preferred_element_type=F32)
        part_ref[:, cols] = total.astype(BF16)

    @pl.loop(0, n_chunks)
    def _(i):
        k_out(i).wait()
        v_out(i).wait()


N_COL = 4


def reduce_kernel(part_ref, x_hbm, out_ref, d_recv, a_send, a_recv, b_send, b_recv, keep, x_ref,
                  x_sem, d_ss, d_rs, a_ss, a_rs, b_ss, b_rs, gb_ss, gb_rs, ga_ss, ga_rs, gd_ss, gd_rs):
    me = lax.axis_index('tp')
    core = me & 1
    xpos = (me >> 1) & 1
    ypos = (me >> 2) & 1
    first_bit = jnp.where(core == 0, 2, 4)
    second_bit = 6 - first_bit
    first = me ^ first_bit
    second = me ^ second_bit
    partner = me ^ 1
    first_pos = jnp.where(core == 0, xpos, ypos)
    second_pos = jnp.where(core == 0, ypos, xpos)
    n_rows, d_model = part_ref.shape
    half, quarter, eighth = n_rows // 2, n_rows // 4, n_rows // 8
    width = d_model // N_COL

    def rows(start, size):
        return pl.ds(pl.multiple_of(start, eighth), size)

    def cols(j):
        return pl.ds(j * width, width)

    mine_half = core * half
    mine_quarter = mine_half + first_pos * quarter
    mine = mine_quarter + second_pos * eighth
    their_quarter = mine_half + (1 - first_pos) * quarter
    second_rows = mine_quarter + (1 - second_pos) * eighth

    def remote(src, dst, ss, rs, dev):
        return pltpu.make_async_remote_copy(src_ref=src, dst_ref=dst, send_sem=ss, recv_sem=rs, device_id={'tp': dev}, device_id_type=MESH)

    x_copy = pltpu.make_async_copy(x_hbm.at[rows(mine, eighth)], x_ref, x_sem)
    x_copy.start()
    barrier = pltpu.get_barrier_semaphore()
    for dev in (partner, first, second):
        pl.semaphore_signal(barrier, inc=1, device_id={'tp': dev}, device_id_type=MESH)
    pl.semaphore_wait(barrier, 3)

    d_copies, a_copies, b_copies = [], [], []
    for j in range(N_COL):
        c = remote(part_ref.at[rows((1 - core) * half, half), cols(j)], d_recv.at[:, cols(j)], d_ss.at[j], d_rs.at[j], partner)
        c.start()
        d_copies.append(c)
    for j in range(N_COL):
        d_copies[j].wait_recv()
        go = part_ref[rows(their_quarter, quarter), cols(j)].astype(F32) + d_recv[rows((1 - first_pos) * quarter, quarter), cols(j)].astype(F32)
        a_send[:, cols(j)] = go.astype(BF16)
        c = remote(a_send.at[:, cols(j)], a_recv.at[:, cols(j)], a_ss.at[j], a_rs.at[j], first)
        c.start()
        a_copies.append(c)
        keep[:, cols(j)] = part_ref[rows(mine_quarter, quarter), cols(j)].astype(F32) + d_recv[rows(first_pos * quarter, quarter), cols(j)].astype(F32)
    for j in range(N_COL):
        a_copies[j].wait_recv()
        away = rows((1 - second_pos) * eighth, eighth)
        b_send[:, cols(j)] = (keep[away, cols(j)] + a_recv[away, cols(j)].astype(F32)).astype(BF16)
        c = remote(b_send.at[:, cols(j)], b_recv.at[:, cols(j)], b_ss.at[j], b_rs.at[j], second)
        c.start()
        b_copies.append(c)
    x_copy.wait()
    gathers = []
    for j in range(N_COL):
        b_copies[j].wait_recv()
        home = rows(second_pos * eighth, eighth)
        total = keep[home, cols(j)] + a_recv[home, cols(j)].astype(F32) + b_recv[:, cols(j)].astype(F32) + x_ref[:, cols(j)].astype(F32)
        out_ref[rows(mine, eighth), cols(j)] = total.astype(BF16)
        block = out_ref.at[rows(mine, eighth), cols(j)]
        sends = [remote(block, block, gb_ss.at[j], gb_rs.at[j], second),
                 remote(block, block, ga_ss.at[j, 0], ga_rs.at[j, 0], first),
                 remote(block, block, gd_ss.at[j, 0], gd_rs.at[j, 0], partner)]
        for c in sends:
            c.start()
        gathers.append(sends)
    for j in range(N_COL):
        gathers[j][0].wait_recv()
        block = out_ref.at[rows(second_rows, eighth), cols(j)]
        sends = [remote(block, block, ga_ss.at[j, 1], ga_rs.at[j, 1], first),
                 remote(block, block, gd_ss.at[j, 1], gd_rs.at[j, 1], partner)]
        for c in sends:
            c.start()
        gathers[j] += sends
    for j in range(N_COL):
        gathers[j][1].wait_recv()
        gathers[j][3].wait_recv()
        block = out_ref.at[rows(their_quarter, quarter), cols(j)]
        c = remote(block, block, gd_ss.at[j, 2], gd_rs.at[j, 2], partner)
        c.start()
        gathers[j].append(c)
    for j in range(N_COL):
        gathers[j][2].wait_recv()
        gathers[j][4].wait_recv()
        gathers[j][5].wait_recv()
    for j in range(N_COL):
        d_copies[j].wait_send()
        a_copies[j].wait_send()
        b_copies[j].wait_send()
        for c in gathers[j]:
            c.wait_send()


def solution(mesh):
    row_spec = P('dp', None)
    vec_spec = P(None)
    cache_spec = P('dp', 'tp', None, None)
    hbm = pl.BlockSpec(memory_space=pl.ANY)
    vmem = pl.BlockSpec(memory_space=pltpu.VMEM)
    dma = pltpu.SemaphoreType.DMA

    def device_step(x, ln_attn_gamma, ln_attn_beta, ln_mlp_gamma, ln_mlp_beta, w_qkv, w_out, w_up, w_down, k_cache, v_cache, positions):
        n_rows, d_model = x.shape
        n_groups, seq, head = k_cache.shape[1:]
        ff = w_up.shape[1]
        n_chunks = n_rows // ROWS
        qkv_cols = n_groups * 3 * head
        freq = ROPE_BASE ** (-2.0 * np.arange(head // 2, dtype=np.float64) / head)
        freq = jnp.asarray(np.concatenate([freq, freq])[None, :], F32)
        w_rows = w_qkv.transpose(0, 2, 1, 3).reshape(d_model * n_groups * 3, head)
        lns = [v.reshape(1, d_model) for v in (ln_attn_gamma, ln_attn_beta, ln_mlp_gamma, ln_mlp_beta)]
        part, k_new, v_new = pl.pallas_call(
            layer_kernel,
            out_shape=(pltpu.VMEM((n_rows, d_model), BF16),
                       jax.ShapeDtypeStruct(k_cache.shape, k_cache.dtype),
                       jax.ShapeDtypeStruct(v_cache.shape, v_cache.dtype)),
            in_specs=[hbm] * 13,
            out_specs=(vmem, hbm, hbm),
            scratch_shapes=[
                pltpu.VMEM((n_rows, d_model), BF16),
                pltpu.VMEM((4, 1, d_model), F32),
                pltpu.VMEM((1, head), F32),
                pltpu.VMEM(w_rows.shape, BF16),
                pltpu.VMEM((d_model, qkv_cols), BF16),
                pltpu.VMEM((n_groups * head, d_model), BF16),
                pltpu.VMEM((d_model, ff), BF16),
                pltpu.VMEM((ff, d_model), BF16),
                pltpu.VMEM(k_cache.shape, BF16),
                pltpu.VMEM(v_cache.shape, BF16),
                pltpu.SMEM((n_rows,), jnp.int32),
                pltpu.VMEM((n_rows, d_model), BF16),
                pltpu.VMEM((n_rows, d_model), BF16),
                pltpu.VMEM((n_rows, qkv_cols), F32),
                pltpu.VMEM((n_rows, 128), jnp.int32),
                pltpu.VMEM((n_groups, n_rows, head), F32),
                pltpu.VMEM((n_groups, n_rows, head), F32),
                pltpu.VMEM((n_groups, n_rows, head), F32),
                pltpu.VMEM((2, n_groups, ROWS, seq), F32),
                pltpu.VMEM((n_rows, n_groups * head), BF16),
                pltpu.VMEM((n_rows, ff), BF16),
                pltpu.VMEM((64 * 3 * n_groups, head), F32),
                dma((8,)), dma((8,)), dma((n_chunks,)), dma((n_chunks,)), dma((n_chunks,)), dma((n_chunks,)),
            ],
            compiler_params=pltpu.CompilerParams(vmem_limit_bytes=60 * 1024 * 1024),
            cost_estimate=pl.CostEstimate(flops=4 * 10 ** 9, bytes_accessed=80 * 10 ** 6, transcendentals=0),
            name='layer',
        )(x, *lns, freq, w_rows, w_out.reshape(n_groups * head, d_model), w_up, w_down, k_cache, v_cache, positions)
        half, quarter, eighth = n_rows // 2, n_rows // 4, n_rows // 8
        out = pl.pallas_call(
            reduce_kernel,
            out_shape=jax.ShapeDtypeStruct((n_rows, d_model), BF16),
            in_specs=[vmem, hbm],
            out_specs=vmem,
            scratch_shapes=[
                pltpu.VMEM((half, d_model), BF16),
                pltpu.VMEM((quarter, d_model), BF16),
                pltpu.VMEM((quarter, d_model), BF16),
                pltpu.VMEM((eighth, d_model), BF16),
                pltpu.VMEM((eighth, d_model), BF16),
                pltpu.VMEM((quarter, d_model), F32),
                pltpu.VMEM((eighth, d_model), BF16),
                dma(()),
                dma((N_COL,)), dma((N_COL,)), dma((N_COL,)), dma((N_COL,)), dma((N_COL,)), dma((N_COL,)),
                dma((N_COL,)), dma((N_COL,)), dma((N_COL, 2)), dma((N_COL, 2)), dma((N_COL, 3)), dma((N_COL, 3)),
            ],
            compiler_params=pltpu.CompilerParams(collective_id=0, has_side_effects=True, vmem_limit_bytes=16 * 1024 * 1024),
            name='reduce',
        )(part, x)
        return out, k_new, v_new

    return jax.shard_map(device_step, mesh=mesh, in_specs=(row_spec, vec_spec, vec_spec, vec_spec, vec_spec, P(None, 'tp', None, None), P('tp', None, None, None), P(None, 'tp'), P('tp', None), cache_spec, cache_spec, P('dp')), out_specs=(row_spec, cache_spec, cache_spec), check_vma=False)
```

time: 146 us -> 61.3 us (0.42)
  Pallas kernels: 0 us -> 59.5 us
  waiting for transfers between devices: 56.8 us -> 0 us
  matrix products: 33.8 us -> 0 us
  other arithmetic: 31.5 us -> 0 us
  between operations: 14.2 us -> 0.67 us
  local copies, waits for them, and re-layouts: 9.15 us -> 0.98 us
    pallas_call x0 -> x2, Pallas kernels: none -> 59.5 us  [the longest x1 38.9 us: device_step(): pl.pallas_call(layer_kernel, out_shape=(pltpu.VMEM((n_rows, d_model), BF1...]
    psum x1 -> x0, waiting for transfers between devices: 56.7 us -> none  [device_step(): mlp_total = lax.psum(mlp_part, 'tp')]
    dot_general x4 -> x0, matrix products: 30.8 us -> none  [the longest x1 12.2 us: attend_local(): jnp.einsum('bgqh,bgsh->bgqs', queries, keys_all, preferred_element_type=j...]
    select_n x1 -> x0, other arithmetic: 23 us -> none  [attend_local(): keys_all = jnp.where(write_mask, new_key[:, :, None, :], k_cache)]
    unnamed x13 -> x3, local copies, waits for them, and re-layouts: 8.76 us -> 0.98 us
    convert_element_type x4 -> x0, other arithmetic: 3.92 us -> none  [the longest x1 3.05 us: device_step(): (x.astype(jnp.float32) + attn_total.astype(jnp.float32) + mlp_total.astyp...]
    reduce_sum x2 -> x0, other arithmetic: 3.09 us -> none  [the longest x1 1.64 us: layer_norm(): row_var = jnp.mean(centred * centred, axis=-1, keepdims=True)]
    unnamed x1 -> x0, matrix products: 3.04 us -> none
  transfers between devices with their start and end apart: 1 -> 0, of which waited for: 1 -> 0; matrix products, arithmetic and copies ran while one was open for 0% -> 0% of each run, Pallas kernels for 0% -> 0%
where the time goes in v1:
time: 61.3 us; the launch traced here: 61.1 us
  Pallas kernels  59.5 us (97%)
  local copies, waits for them, and re-layouts  0.98 us (2%)
  between operations  0.67 us (1%)
    pallas_call x1, Pallas kernels, device_step(): pl.pallas_call(layer_kernel, out_shape=(pltpu.VMEM((n_rows, d_model), BF1...  38.9 us
    pallas_call x1, Pallas kernels, device_step(): pl.pallas_call(reduce_kernel, out_shape=jax.ShapeDtypeStruct((n_rows, d_m...  20.6 us

profile of v1, /device:TPU:0, one launch (start us, length us, event | category | flops | bytes accessed | tf_op | source)
XLA Modules:
  0.0 61.1 jit_solution(11193869507652553629)
XLA Ops:
  0.6 0.0 copy-start
  0.6 38.9 %layer.1 = (bf16[256,2048]{1,0:T(8,128)(2,1)S(1)}, bf16[256,2,128,128]{3,2,1,0:T(8,128)(2,1)}, bf16[256,2,128,128]{3,2,1,0:T(8,128)(2,1)}) custom-call(bf16[256,2048]{1,0:T(8,128)(2,1)} %x_hbm.3, f32[1,2048]{1,0:T(1,128)} %bitcast.10, f32[1,2048]{1,0:T(1,128)} %bitcast.11, f32[1,2048]{1,0:T(1,128)} %bitcast.12, f32[1,2048]{1,0:T(1,128)} %bitcast.13, ...), custom_call_target="tpu_custom_call" | custom-call | flops 4000000000 | bytes 80000000 | tf_op jit(solution)/shard_map/layer/pallas_call | solution.py:340
  39.6 0.0 copy-done
  39.6 20.6 %reduce.1 = bf16[256,2048]{1,0:T(8,128)(2,1)S(1)} custom-call(bf16[256,2048]{1,0:T(8,128)(2,1)S(1)} %get-tuple-element.6.part_ref, bf16[256,2048]{1,0:T(8,128)(2,1)S(1)} %copy-done), custom_call_target="tpu_custom_call" | custom-call | tf_op jit(solution)/shard_map/reduce/pallas_call | solution.py:377
  60.2 1.0 %copy.17 = bf16[256,2048]{1,0:T(8,128)(2,1)} copy(bf16[256,2048]{1,0:T(8,128)(2,1)S(1)} %reduce.1) | data formatting | bytes 2097152
Async XLA Ops:
  0.6 39.0 %copy-start = (bf16[256,2048]{1,0:T(8,128)(2,1)S(1)}, bf16[256,2048]{1,0:T(8,128)(2,1)}, u32[]{:S(2)}) copy-start(bf16[256,2048]{1,0:T(8,128)(2,1)} %x_hbm.3) | copy-start | bytes 3145732

commit v2 on v1

--- a/solution.py
+++ b/solution.py
@@ -71,14 +71,16 @@
     def v_out(i):
         return pltpu.make_async_copy(vbuf.at[chunk_ds(i)], vo_hbm.at[chunk_ds(i)], sem_vo.at[i])
 
-    for i in range(n_chunks):
-        k_in(i).start()
-        v_in(i).start()
+    def fetch(lo, hi):
+        @pl.loop(lo, hi)
+        def _(i):
+            k_in(i).start()
+            v_in(i).start()
+
+    fetch(0, 2)
     wbig = [pltpu.make_async_copy(wup_hbm, wup_ref, sem_w.at[n_wparts]),
             pltpu.make_async_copy(wdown_hbm, wdown_ref, sem_w.at[n_wparts + 1]),
             pltpu.make_async_copy(wout_hbm, wout_ref, sem_w.at[n_wparts + 2])]
-    for c in wbig:
-        c.start()
 
     smalls[0].wait()
     row8 = lax.broadcasted_iota(jnp.int32, (8, 128), 0)
@@ -92,6 +94,7 @@
 
     for c in smalls[1:]:
         c.wait()
+    fetch(2, 5)
 
     gains = [ln_ref[i] for i in range(4)]
 
@@ -106,6 +109,8 @@
         ain_ref[rows, :] = (normed * gains[0] + gains[1]).astype(BF16)
         min_ref[rows, :] = (normed * gains[2] + gains[3]).astype(BF16)
 
+    fetch(5, 8)
+
     depth = 64
     n_split = 3 * n_groups
     for p in range(n_wparts):
@@ -120,6 +125,12 @@
                 for g in range(n_groups):
                     col = (g * 3 + slot) * 128
                     wcat_ref[feat, col:col + 128] = stage_ref[pl.ds(slot * n_groups + g, depth, stride=n_split), :].astype(BF16)
+
+        fetch(8 + p, 9 + p)
+
+    for c in wbig:
+        c.start()
+    fetch(12, n_chunks)
 
     for c0 in range(0, 3 * n_groups * 128, 256):
         y_ref[:, c0:c0 + 256] = jnp.dot(ain_ref[...], wcat_ref[:, c0:c0 + 256], preferred_element_type=F32).astype(BF16).astype(F32)

time: 61.3 us -> 54.5 us (0.89)
  Pallas kernels: 59.5 us -> 52.7 us
    pallas_call x1, Pallas kernels: 38.9 us -> 32.2 us  [device_step(): pl.pallas_call(layer_kernel, out_shape=(pltpu.VMEM((n_rows, d_model), BF1...]
where the time goes in v2:
time: 54.5 us; the launch traced here: 54.4 us
  Pallas kernels  52.7 us (97%)
  local copies, waits for them, and re-layouts  0.98 us (2%)
  between operations  0.67 us (1%)
    pallas_call x1, Pallas kernels, device_step(): pl.pallas_call(layer_kernel, out_shape=(pltpu.VMEM((n_rows, d_model), BF1...  32.2 us
    pallas_call x1, Pallas kernels, device_step(): pl.pallas_call(reduce_kernel, out_shape=jax.ShapeDtypeStruct((n_rows, d_m...  20.6 us

profile of v2, /device:TPU:0, one launch (start us, length us, event | category | flops | bytes accessed | tf_op | source)
XLA Modules:
  0.0 54.4 jit_solution(3532369732364935178)
XLA Ops:
  0.6 0.0 copy-start
  0.6 32.2 %layer.1 = (bf16[256,2048]{1,0:T(8,128)(2,1)S(1)}, bf16[256,2,128,128]{3,2,1,0:T(8,128)(2,1)}, bf16[256,2,128,128]{3,2,1,0:T(8,128)(2,1)}) custom-call(bf16[256,2048]{1,0:T(8,128)(2,1)} %x_hbm.3, f32[1,2048]{1,0:T(1,128)} %bitcast.10, f32[1,2048]{1,0:T(1,128)} %bitcast.11, f32[1,2048]{1,0:T(1,128)} %bitcast.12, f32[1,2048]{1,0:T(1,128)} %bitcast.13, ...), custom_call_target="tpu_custom_call" | custom-call | flops 4000000000 | bytes 80000000 | tf_op jit(solution)/shard_map/layer/pallas_call | solution.py:351
  32.8 0.0 copy-done
  32.8 20.6 %reduce.1 = bf16[256,2048]{1,0:T(8,128)(2,1)S(1)} custom-call(bf16[256,2048]{1,0:T(8,128)(2,1)S(1)} %get-tuple-element.6.part_ref, bf16[256,2048]{1,0:T(8,128)(2,1)S(1)} %copy-done), custom_call_target="tpu_custom_call" | custom-call | tf_op jit(solution)/shard_map/reduce/pallas_call | solution.py:388
  53.4 1.0 %copy.17 = bf16[256,2048]{1,0:T(8,128)(2,1)} copy(bf16[256,2048]{1,0:T(8,128)(2,1)S(1)} %reduce.1) | data formatting | bytes 2097152
Async XLA Ops:
  0.6 32.2 %copy-start = (bf16[256,2048]{1,0:T(8,128)(2,1)S(1)}, bf16[256,2048]{1,0:T(8,128)(2,1)}, u32[]{:S(2)}) copy-start(bf16[256,2048]{1,0:T(8,128)(2,1)} %x_hbm.3) | copy-start | bytes 3145732
